TPU v7x, 768 devices: a whole 4x8x12 slice. The times are simulated.
768 devices in a mesh: group: 48 (over z, x), fsdp: 4 (over y_hi, core), tensor: 4 (over y_lo).
Axes of the slice: x: 4, y: 8 (y_hi: 2, y_lo: 4; y = y_hi * 4 + y_lo), z: 12, core: 2. Of those that a mesh axis runs over, the one named last changes fastest.
Arguments:
- tokens: bfloat16 [24576, 8192], P(('group', 'fsdp')), may hold values from -6 to 6
- cotangent: bfloat16 [24576, 512], P(('group', 'fsdp'), 'tensor'), may hold values from -0.0390625 to 0.0390625
- weight: bfloat16 [8192, 512], P('fsdp', 'tensor'), may hold values from -0.0625 to 0.0625
- moment_one: float32 [8192, 512], P('fsdp', 'tensor'), may hold values from -4 to 4
- moment_two: float32 [8192, 512], P('fsdp', 'tensor'), may hold values from 0.003 to 0.3
- hidden: bfloat16 [4, 12288, 8192], P(None, 'group', ('fsdp', 'tensor')), may hold values from -6 to 6
- queries: bfloat16 [4, 12288, 4096], P(None, ('group', 'fsdp', 'tensor')), may hold values from -145 to 145
- new_keys: bfloat16 [4, 12288, 512], P(None, ('group', 'fsdp', 'tensor')), may hold values from -4 to 4
- key_cache: bfloat16 [12288, 32, 512], P(('group', 'fsdp', 'tensor')), may hold values from -4 to 4
- value_cache: bfloat16 [12288, 32, 512], P(('group', 'fsdp', 'tensor')), may hold values from -6 to 6
- lengths: int32 [12288], P(('group', 'fsdp', 'tensor')), may hold values from 2 to 32
Outputs:
- new_weight: bfloat16 [8192, 512], P('fsdp', 'tensor')
- new_moment_one: float32 [8192, 512], P('fsdp', 'tensor')
- new_moment_two: float32 [8192, 512], P('fsdp', 'tensor')
- attention: bfloat16 [4, 12288, 4096], P(None, ('group', 'fsdp', 'tensor'))
All inputs are finite; a program needn't handle non-finite values.
Results may differ from a plain program's by a relative error of at most 0.007.
Values may be sent and summed in bfloat16 or wider, within the bound.
No kernel may reach another device: no remote copies, remote signals or barrier semaphores. Data moves between devices by JAX's collectives and lax.ppermute only.
A program may use at most 64 MiB of HBM per device.

v0:
```python
import jax
import jax.numpy as jnp
from jax import lax
from jax.experimental import pallas as pl
from jax.experimental.pallas import tpu as pltpu
from jax.sharding import Mesh
from jax.sharding import PartitionSpec as P

HEAD_DIM = 128
GROUP_HEADS = 8
KV_HEADS = 4
STEPS = 4
ADAM_STEP = 10
GZ, GX, YH, YL, CO = "gz", "gx", "yh", "yl", "co"
GROUP = (GZ, GX)
FSDP = (YH, CO)
ALL = (GZ, GX, YH, CO, YL)
NX, NZ = 4, 12
QROWS = 512
PART = 48
STARTS = tuple(min(PART * k, QROWS - PART) for k in range(NZ))

learn_rate = 0.001
beta_one = 0.9
beta_two = 0.95
epsilon = 1e-08
decay_rate = 0.1
masked_score = -1e30


def apply_adamw(gradient, weight, moment_one, moment_two):
    first_new = beta_one * moment_one + (1.0 - beta_one) * gradient
    second_new = beta_two * moment_two + (1.0 - beta_two) * gradient * gradient
    first_hat = first_new / (1.0 - beta_one**ADAM_STEP)
    second_hat = second_new / (1.0 - beta_two**ADAM_STEP)
    stepped = weight.astype(jnp.float32) * (
        1.0 - learn_rate * decay_rate
    ) - learn_rate * first_hat / (jnp.sqrt(second_hat) + epsilon)
    return (stepped.astype(jnp.bfloat16), first_new, second_new)


def vmem():
    return pl.BlockSpec(memory_space=pltpu.VMEM)


def wide(t):
    return t[0] // 2


def grad_kernel(t, core, own_0, own_1, recv_0, recv_1, cot_0, cot_1, out):
    b = t[0] % 2
    cot = jnp.concatenate([cot_0[...], cot_1[...]], axis=0)
    for rows, (own, recv) in enumerate(((own_0, recv_0), (own_1, recv_1))):
        tok = jnp.concatenate([own[...], recv[...]], axis=0)
        value = lax.dot_general(
            tok, cot, (((0,), (0,)), ((), ())), preferred_element_type=jnp.float32
        ).astype(jnp.bfloat16)
        first = 2 * (core[0] ^ rows)
        out[first + b, 0] = value[:QROWS]
        out[first + (1 - b), 0] = value[QROWS:]


def partial_gradient(t, core, tokens, recv, cot_0, cot_1):
    return pl.pallas_call(
        grad_kernel,
        out_shape=jax.ShapeDtypeStruct((NX, 2, QROWS, 128), jnp.bfloat16),
        grid_spec=pltpu.PrefetchScalarGridSpec(
            num_scalar_prefetch=2,
            grid=(2,),
            in_specs=[
                pl.BlockSpec((128, 1024), lambda i, t, c: (0, 4 * i + wide(t))),
                pl.BlockSpec((128, 1024), lambda i, t, c: (0, 4 * i + 2 + wide(t))),
                pl.BlockSpec((128, 1024), lambda i, t, c: (0, 4 * i + wide(t))),
                pl.BlockSpec((128, 1024), lambda i, t, c: (0, 4 * i + 2 + wide(t))),
                pl.BlockSpec((128, 128), lambda i, t, c: (0, 0)),
                pl.BlockSpec((128, 128), lambda i, t, c: (0, 0)),
            ],
            out_specs=pl.BlockSpec((NX, 1, QROWS, 128), lambda i, t, c: (0, i, 0, 0)),
        ),
        name="partial_gradient",
    )(t, core, tokens, tokens, recv, recv, cot_0, cot_1)


def sum_x_kernel(parts, out):
    total = parts[0].astype(jnp.float32)
    for k in range(1, NX * 2):
        total = total + parts[k].astype(jnp.float32)
    total = total.astype(jnp.bfloat16)
    for z in range(NZ):
        out[z] = total[STARTS[z] : STARTS[z] + PART]


def sum_over_x(parts):
    return pl.pallas_call(
        sum_x_kernel,
        out_shape=jax.ShapeDtypeStruct((NZ, PART, 128), jnp.bfloat16),
        in_specs=[vmem()],
        out_specs=vmem(),
        name="sum_over_x",
    )(parts)


def shard_kernel(parts, state, grad_out, weight_out):
    total = parts[0].astype(jnp.float32)
    for k in range(1, NZ):
        total = total + parts[k].astype(jnp.float32)
    grad_out[...] = total.astype(jnp.bfloat16)
    weight_out[...] = apply_adamw(total, state[0], state[1], state[2])[0]


def update_shard(parts, state):
    return pl.pallas_call(
        shard_kernel,
        out_shape=(jax.ShapeDtypeStruct((PART, 128), jnp.bfloat16),) * 2,
        in_specs=[vmem()] * 2,
        out_specs=(vmem(), vmem()),
        name="update_shard",
    )(parts, state)


def join_kernel(parts, out):
    last = 480 - STARTS[NZ - 2]
    for kind in range(2):
        kept = [parts[z, kind] for z in range(10)] + [parts[NZ - 2, kind, last:]]
        whole = jnp.concatenate(kept, axis=0)
        for k in range(NX):
            out[k, kind] = whole


def join_parts(parts):
    return pl.pallas_call(
        join_kernel,
        out_shape=jax.ShapeDtypeStruct((NX, 2, QROWS, 128), jnp.bfloat16),
        in_specs=[vmem()],
        out_specs=vmem(),
        name="join_parts",
    )(parts)


def adamw_kernel(t, core, grad, weight, one, two, weight_out, one_out, two_out):
    new_weight, first, second = apply_adamw(
        grad[0, 0].astype(jnp.float32), weight[...], one[...], two[...]
    )
    weight_out[...] = new_weight
    one_out[...] = first
    two_out[...] = second


def update_all(t, core, both, weight, one, two):
    block = pl.BlockSpec(
        (QROWS, 128), lambda k, t, c: (t[0] ^ (2 * (c[0] ^ (k // 2))) ^ (k % 2), 0)
    )
    grad = pl.BlockSpec((1, 1, QROWS, 128), lambda k, t, c: (k, 1, 0, 0))
    shape = lambda d: jax.ShapeDtypeStruct((2048, 128), d)
    return pl.pallas_call(
        adamw_kernel,
        out_shape=(shape(jnp.bfloat16), shape(jnp.float32), shape(jnp.float32)),
        grid_spec=pltpu.PrefetchScalarGridSpec(
            num_scalar_prefetch=2,
            grid=(NX,),
            in_specs=[grad, block, block, block],
            out_specs=(block, block, block),
        ),
        name="update_all",
    )(t, core, both, weight, one, two)


def values_kernel(parts, own, near, far_own, far_near, out):
    value = None
    for p, rows in enumerate((own, near, far_own, far_near)):
        part = jnp.dot(rows[0], parts[p, 0], preferred_element_type=jnp.float32)
        value = part if value is None else value + part
    value = value.astype(jnp.bfloat16)
    for d in range(16):
        out[d] = value[d * 16 : (d + 1) * 16]


def values_part(both, own, near, far_own, far_near):
    rows = pl.BlockSpec((1, 256, 512), lambda s: (s, 0, 0))
    return pl.pallas_call(
        values_kernel,
        out_shape=jax.ShapeDtypeStruct((16, STEPS * 16, 128), jnp.bfloat16),
        grid=(STEPS,),
        in_specs=[
            pl.BlockSpec((NX, 1, QROWS, 128), lambda s: (0, 0, 0, 0)),
            rows,
            rows,
            rows,
            rows,
        ],
        out_specs=pl.BlockSpec((16, 16, 128), lambda s: (0, s, 0)),
        name="values_part",
    )(both, own, near, far_own, far_near)


def attend_cached(queries, new_keys, key_cache, lengths):
    row_total = lengths.shape[0]
    cache_len = key_cache.shape[1]
    query_b = queries.reshape(STEPS, row_total, KV_HEADS, GROUP_HEADS, HEAD_DIM)
    cached_keys = key_cache.reshape(row_total, cache_len, KV_HEADS, HEAD_DIM)
    fresh_keys = new_keys.reshape(STEPS, row_total, KV_HEADS, HEAD_DIM)
    score_scale = HEAD_DIM ** (-0.5)
    cached_scores = (
        jnp.einsum("tnhjd,nphd->nhjtp", query_b, cached_keys, preferred_element_type=jnp.float32)
        * score_scale
    )
    fresh_scores = (
        jnp.einsum("tnhjd,snhd->nhjts", query_b, fresh_keys, preferred_element_type=jnp.float32)
        * score_scale
    )
    cached_valid = jnp.arange(cache_len, dtype=jnp.int32)[None, :] < lengths[:, None]
    fresh_valid = (
        jnp.arange(STEPS, dtype=jnp.int32)[None, :] <= jnp.arange(STEPS, dtype=jnp.int32)[:, None]
    )
    cached_scores = jnp.where(cached_valid[:, None, None, None, :], cached_scores, masked_score)
    fresh_scores = jnp.where(fresh_valid[None, None, None, :, :], fresh_scores, masked_score)
    highest = jnp.maximum(jnp.max(cached_scores, axis=-1), jnp.max(fresh_scores, axis=-1))[
        ..., None
    ]
    cached_exp = jnp.exp(cached_scores - highest)
    fresh_exp = jnp.exp(fresh_scores - highest)
    denominator = jnp.sum(cached_exp, axis=-1, keepdims=True) + jnp.sum(
        fresh_exp, axis=-1, keepdims=True
    )
    cached_probs = (cached_exp / denominator).astype(jnp.bfloat16)
    fresh_probs = (fresh_exp / denominator).astype(jnp.bfloat16)
    return cached_probs, fresh_probs


def spread_probs(fresh_probs):
    row_total = fresh_probs.shape[0]
    spread = jnp.transpose(fresh_probs, (1, 2, 3, 0, 4))[..., None]
    same = jnp.eye(row_total, dtype=jnp.bool_)[None, None, None, :, None, :]
    spread = jnp.where(same, spread, jnp.zeros((), jnp.bfloat16))
    return spread.reshape(KV_HEADS, -1, STEPS * row_total)


def weigh_cached(cached_probs, value_cache):
    cached_values = value_cache.reshape(*value_cache.shape[:2], KV_HEADS, HEAD_DIM)
    return jnp.einsum(
        "nhjtp,nphd->hjtnd", cached_probs, cached_values, preferred_element_type=jnp.float32
    ).reshape(KV_HEADS, -1, HEAD_DIM)


def finish_kernel(values, result, spread, out):
    for h in range(KV_HEADS):
        total = None
        for k in range(2):
            for c in range(2):
                for v in (h & 1, (h & 1) + 2):
                    if (v ^ (2 * c)) == h:
                        part = values[k * 8 + c * 4 + v].astype(jnp.float32)
                        total = part if total is None else total + part
        value = result[h] + jnp.dot(
            spread[h], total.astype(jnp.bfloat16), preferred_element_type=jnp.float32
        )
        value = value.astype(jnp.bfloat16)
        for j in range(GROUP_HEADS):
            first = (h * GROUP_HEADS + j) * HEAD_DIM
            out[:, first : first + HEAD_DIM] = value[j * 64 : (j + 1) * 64]


def finish_attention(values, result, spread):
    return pl.pallas_call(
        finish_kernel,
        out_shape=jax.ShapeDtypeStruct((64, 4096), jnp.bfloat16),
        in_specs=[vmem()] * 3,
        out_specs=vmem(),
        name="finish_attention",
    )(values, result, spread)


def per_device(
    tokens,
    cotangent,
    weight,
    moment_one,
    moment_two,
    hidden,
    queries,
    new_keys,
    key_cache,
    value_cache,
    lengths,
):
    c, y = lax.axis_index(CO), lax.axis_index(YL)
    x, z = lax.axis_index(GX), lax.axis_index(GZ)
    core, t = c.astype(jnp.int32).reshape(1), y.astype(jnp.int32).reshape(1)
    swap = [(0, 1), (1, 0)]
    spots = [(k, v) for k in range(2) for v in range(4)]
    bring = [[((k ^ j) * 4 + (v ^ (2 * k)), k * 4 + v) for k, v in spots] for j in range(2)]

    cots = [lax.ppermute(cotangent, (CO, YL), pairs) for pairs in bring]
    recv = lax.ppermute(tokens, CO, swap)
    parts = partial_gradient(t, core, tokens, recv, *cots)
    early = (weight, moment_one, moment_two)
    queries, new_keys, key_cache, early, parts = lax.optimization_barrier(
        (queries, new_keys, key_cache, early, parts)
    )
    parts = lax.all_to_all(parts.reshape(NX * 2, QROWS, 128), (GX, YH), 0, 0, tiled=True)

    j, i = x // 2, x % 2
    first = (y ^ (2 * (c ^ j)) ^ i) * QROWS + jnp.minimum(PART * z, QROWS - PART)
    state = jnp.stack(
        [lax.dynamic_slice_in_dim(v, first, PART, 0).astype(jnp.float32) for v in early]
    )
    turn = [(v * 8 + s, v * 8 + d) for v in range(NX) for s, d in bring[v // 2]]
    back = [(d, s) for s, d in turn]
    state = lax.ppermute(state, (GX, CO, YL), turn)

    far = lax.ppermute(hidden, CO, swap)
    cached_probs, fresh_probs = attend_cached(queries, new_keys, key_cache, lengths)
    spread = spread_probs(fresh_probs)
    parts = sum_over_x(parts)
    parts = lax.all_to_all(parts, GZ, 0, 0, tiled=True)
    parts, state, cached_probs, spread = lax.optimization_barrier(
        (parts, state, cached_probs, spread)
    )
    grad, shard = update_shard(parts, state)

    grad = lax.ppermute(grad, (GX, CO, YL), back)
    both = jnp.broadcast_to(jnp.stack([shard, grad])[None], (NZ, 2, PART, 128))
    both = lax.all_to_all(both, GZ, 0, 0, tiled=True)
    near = lax.ppermute(hidden, YL, [(0, 1), (1, 0), (2, 3), (3, 2)])
    result = weigh_cached(cached_probs, value_cache)
    both = join_parts(both)
    both = lax.all_to_all(both, GX, 0, 0, tiled=True)
    far_near = lax.ppermute(near, CO, swap)
    both, result = lax.optimization_barrier((both, result))
    values = values_part(both, hidden, near, far, far_near)
    values = lax.all_to_all(values, (YH, CO, YL), 0, 0, tiled=True)
    new_weight, first_new, second_new = update_all(t, core, both, weight, moment_one, moment_two)
    attention = finish_attention(values, result, spread).reshape(STEPS, 16, 4096)
    return (new_weight, first_new, second_new, attention)


def solution(mesh):
    split = Mesh(mesh.devices.reshape(NZ, NX, 2, 2, 4), (GZ, GX, YH, CO, YL))
    rows, cols = FSDP, YL
    return jax.shard_map(
        per_device,
        mesh=split,
        in_specs=(
            P(GROUP + FSDP, None),
            P(GROUP + FSDP, cols),
            P(rows, cols),
            P(rows, cols),
            P(rows, cols),
            P(None, GROUP, FSDP + (YL,)),
            P(None, ALL, None),
            P(None, ALL, None),
            P(ALL, None, None),
            P(ALL, None, None),
            P(ALL),
        ),
        out_specs=(P(rows, cols), P(rows, cols), P(rows, cols), P(None, ALL, None)),
        check_vma=False,
    )
```

profile of v0, /device:TPU:73, one launch (start us, length us, event | category | flops | bytes accessed | tf_op | source)
XLA Modules:
  0.0 171.0 jit_solution(7358275173585946090)
XLA Ops:
  0.6 2.6 %collective-permute-start = (bf16[128,8192]{1,0:T(8,128)(2,1)}, bf16[128,8192]{1,0:T(8,128)(2,1)S(1)}, u32[]{:S(2)}, u32[]{:S(2)}) collective-permute-start(bf16[128,8192]{1,0:T(8,128)(2,1)} %own_1.1), channel_id=1, source_target_pairs={{0,4},{4,0},{1,5},{5,1},{2,6},{6,2},{3,7},{7,3},{8,12},{12,8},{9,1... | collective-permute-start | bytes 6291464 | tf_op jit(solution)/shard_map/ppermute | solution.py:294
  3.2 4.2 %collective-permute-start.1 = (bf16[128,128]{1,0:T(8,128)(2,1)}, bf16[128,128]{1,0:T(8,128)(2,1)S(1)}, u32[]{:S(2)}, u32[]{:S(2)}) collective-permute-start(bf16[128,128]{1,0:T(8,128)(2,1)} %param.12), channel_id=1, source_target_pairs={{0,0},{1,1},{2,2},{3,3},{6,4},{7,5},{4,6},{5,7},{8,8},{9,9},{10,10... | collective-permute-start | bytes 98312 | tf_op jit(solution)/shard_map/ppermute | solution.py:293
  7.4 1.9 %collective-permute-start.2 = (bf16[128,128]{1,0:T(8,128)(2,1)}, bf16[128,128]{1,0:T(8,128)(2,1)S(1)}, u32[]{:S(2)}, u32[]{:S(2)}) collective-permute-start(bf16[128,128]{1,0:T(8,128)(2,1)} %param.12), channel_id=1, source_target_pairs={{4,0},{5,1},{6,2},{7,3},{2,4},{3,5},{0,6},{1,7},{12,8},{13,9},{14,... | collective-permute-start | bytes 98312 | tf_op jit(solution)/shard_map/ppermute | solution.py:293
  9.4 2.1 %collective-permute-start.5 = (bf16[4,256,512]{2,1,0:T(8,128)(2,1)}, bf16[4,256,512]{2,1,0:T(8,128)(2,1)}, u32[]{:S(2)}, u32[]{:S(2)}) collective-permute-start(bf16[4,256,512]{2,1,0:T(8,128)(2,1)} %own.1), channel_id=1, source_target_pairs={{0,1},{1,0},{2,3},{3,2},{4,5},{5,4},{6,7},{7,6},{8,9},{9,8},{10,11... | collective-permute-start | bytes 3145736 | tf_op jit(solution)/shard_map/ppermute | solution.py:324
  15.5 3.1 %partial_gradient.1 = bf16[4,2,512,128]{3,2,1,0:T(8,128)(2,1)} custom-call(s32[1]{0:T(128)} %bitcast.t, s32[1]{0:T(128)} %bitcast.1.core, bf16[128,8192]{1,0:T(8,128)(2,1)} %own_1.1, bf16[128,8192]{1,0:T(8,128)(2,1)} %own_1.1, bf16[128,8192]{1,0:T(8,128)(2,1)} %copy-done.1, bf16[128,8192]{1,0:T(8,128)(2,1)} %copy-done.1, bf16[128,128]{1,0:T(8,128)(2,1)} %copy-done.11, ...), custom_call_target="tpu_custom_call" | custom-call | tf_op jit(solution)/shard_map/partial_gradient/pallas_call | solution.py:64
  18.6 6.9 %all-to-all-start = ((bf16[8,512,128]{2,1,0:T(8,128)(2,1)}), bf16[8,512,128]{2,1,0:T(8,128)(2,1)S(1)}, u32[]{:S(2)}, u32[]{:S(2)}) async-start(bf16[8,512,128]{2,1,0:T(8,128)(2,1)} %bitcast.47), calls=%async_computation | async-start | bytes 2097152 | tf_op jit(solution)/shard_map/all_to_all | solution.py:300
  25.7 2.4 %fusion.6 = f32[16,4,4,4,8]{4,2,3,1,0:T(4,128)S(1)} fusion(bf16[4,16,4,8,128]{4,3,2,1,0:T(8,128)(2,1)S(1)} %bitcast.50, bf16[4,16,4,128,1]{3,2,1,0,4:T(4,128)(2,1)S(1)} %bitcast.57), kind=kOutput, calls=%fused_computation.11 | convolution fusion | flops 2097152 | bytes 622592 | tf_op jit(solution)/shard_map/tnhjd,snhd->nhjts/dot_general | solution.py:208
  29.5 1.6 fusion.15
  34.2 26.7 %all-to-all-done.parts = bf16[8,512,128]{2,1,0:T(8,128)(2,1)S(1)} async-done(((bf16[8,512,128]{2,1,0:T(8,128)(2,1)}), bf16[8,512,128]{2,1,0:T(8,128)(2,1)S(1)}, u32[]{:S(2)}, u32[]{:S(2)}) %all-to-all-start) | async-done | bytes 1048608 | tf_op jit(solution)/shard_map/all_to_all | solution.py:300
  60.9 1.0 copy-done.2
  61.9 2.0 %sum_over_x.1 = bf16[12,48,128]{2,1,0:T(8,128)(2,1)} custom-call(bf16[8,512,128]{2,1,0:T(8,128)(2,1)} %copy-done.2), custom_call_target="tpu_custom_call" | custom-call | tf_op jit(solution)/shard_map/sum_over_x/pallas_call | solution.py:94
  63.9 14.2 %all-to-all-start.1 = ((bf16[12,48,128]{2,1,0:T(8,128)(2,1)}), bf16[12,48,128]{2,1,0:T(8,128)(2,1)S(1)}, u32[]{:S(2)}, u32[]{:S(2)}) async-start(bf16[12,48,128]{2,1,0:T(8,128)(2,1)} %sum_over_x.1), calls=%async_computation.1 | async-start | bytes 294912 | tf_op jit(solution)/shard_map/all_to_all | solution.py:315
  79.5 3.6 %broadcast_in_dim.81 = bf16[4,512,64]{1,2,0:T(8,128)(2,1)S(1)} reshape(bf16[4,8,4,16,4,16]{3,2,1,5,4,0:T(4,128)(2,1)S(1)} %broadcast_in_dim.80) | data formatting | bytes 524288 | tf_op jit(solution)/shard_map/jit(_where)/broadcast_in_dim | solution.py:234
  83.4 1.9 %collective-permute-start.3 = (f32[3,48,128]{2,1,0:T(8,128)S(1)}, f32[3,48,128]{2,1,0:T(8,128)S(1)}, u32[]{:S(2)}, u32[]{:S(2)}) collective-permute-start(f32[3,48,128]{2,1,0:T(8,128)S(1)} %pad_maximum_fusion), channel_id=1, source_target_pairs={{0,0},{1,1},{2,2},{3,3},{6,4},{7,5},{4,6},{5,7},{16,16},{17,17},{1... | collective-permute-start | bytes 221192 | tf_op jit(solution)/shard_map/ppermute | solution.py:309
  86.2 3.4 %collective-permute-done.3.state = f32[3,48,128]{2,1,0:T(8,128)S(1)} collective-permute-done((f32[3,48,128]{2,1,0:T(8,128)S(1)}, f32[3,48,128]{2,1,0:T(8,128)S(1)}, u32[]{:S(2)}, u32[]{:S(2)}) %collective-permute-start.3) | collective-permute-done | bytes 73760 | tf_op jit(solution)/shard_map/ppermute | solution.py:309
  90.9 1.6 update_shard.1
  92.5 2.0 %collective-permute-start.4 = (bf16[48,128]{1,0:T(8,128)(2,1)}, bf16[48,128]{1,0:T(8,128)(2,1)S(1)}, u32[]{:S(2)}, u32[]{:S(2)}) collective-permute-start(bf16[48,128]{1,0:T(8,128)(2,1)} %get-tuple-element.32), channel_id=1, source_target_pairs={{0,0},{1,1},{2,2},{3,3},{4,6},{5,7},{6,4},{7,5},{16,16},{17,17},{1... | collective-permute-start | bytes 36872 | tf_op jit(solution)/shard_map/ppermute | solution.py:321
  94.5 3.5 %collective-permute-done.4 = bf16[48,128]{1,0:T(8,128)(2,1)S(1)} collective-permute-done((bf16[48,128]{1,0:T(8,128)(2,1)}, bf16[48,128]{1,0:T(8,128)(2,1)S(1)}, u32[]{:S(2)}, u32[]{:S(2)}) %collective-permute-start.4) | collective-permute-done | bytes 12320 | tf_op jit(solution)/shard_map/ppermute | solution.py:321
  99.5 8.9 %all-to-all-start.2 = ((bf16[12,2,48,128]{3,2,1,0:T(8,128)(2,1)}), bf16[12,2,48,128]{3,2,1,0:T(8,128)(2,1)S(1)}, u32[]{:S(2)}, u32[]{:S(2)}) async-start(bf16[12,2,48,128]{3,2,1,0:T(8,128)(2,1)} %broadcast_in_dim.83), calls=%async_computation.2 | async-start | bytes 589824 | tf_op jit(solution)/shard_map/all_to_all | solution.py:323
  108.4 1.9 %collective-permute-start.6 = (bf16[4,256,512]{2,1,0:T(8,128)(2,1)}, bf16[4,256,512]{2,1,0:T(8,128)(2,1)S(1)}, u32[]{:S(2)}, u32[]{:S(2)}) collective-permute-start(bf16[4,256,512]{2,1,0:T(8,128)(2,1)} %own.1), channel_id=1, source_target_pairs={{0,4},{4,0},{1,5},{5,1},{2,6},{6,2},{3,7},{7,3},{8,12},{12,8},{9,1... | collective-permute-start | bytes 3145736 | tf_op jit(solution)/shard_map/ppermute | solution.py:311
  110.3 2.4 %collective-permute-start.7 = (bf16[4,256,512]{2,1,0:T(8,128)(2,1)}, bf16[4,256,512]{2,1,0:T(8,128)(2,1)}, u32[]{:S(2)}, u32[]{:S(2)}) collective-permute-start(bf16[4,256,512]{2,1,0:T(8,128)(2,1)} %collective-permute-done.5.near), channel_id=1, source_target_pairs={{0,4},{4,0},{1,5},{5,1},{2,6},{6,2},{3,7},{7,3},{8,12},{12,8},{9,1... | collective-permute-start | bytes 3145736 | tf_op jit(solution)/shard_map/ppermute | solution.py:328
  112.7 8.7 %all-to-all-done.2.parts = bf16[12,2,48,128]{3,2,1,0:T(8,128)(2,1)S(1)} async-done(((bf16[12,2,48,128]{3,2,1,0:T(8,128)(2,1)}), bf16[12,2,48,128]{3,2,1,0:T(8,128)(2,1)S(1)}, u32[]{:S(2)}, u32[]{:S(2)}) %all-to-all-start.2) | async-done | bytes 294944 | tf_op jit(solution)/shard_map/all_to_all | solution.py:323
  122.2 2.1 %join_parts.1 = bf16[4,2,512,128]{3,2,1,0:T(8,128)(2,1)} custom-call(bf16[12,2,48,128]{3,2,1,0:T(8,128)(2,1)} %copy-done.3), custom_call_target="tpu_custom_call" | custom-call | tf_op jit(solution)/shard_map/join_parts/pallas_call | solution.py:131
  124.2 6.7 %all-to-all-start.3 = ((bf16[4,2,512,128]{3,2,1,0:T(8,128)(2,1)}), bf16[4,2,512,128]{3,2,1,0:T(8,128)(2,1)S(1)}, u32[]{:S(2)}, u32[]{:S(2)}) async-start(bf16[4,2,512,128]{3,2,1,0:T(8,128)(2,1)} %join_parts.1), calls=%async_computation.3 | async-start | bytes 2097152 | tf_op jit(solution)/shard_map/all_to_all | solution.py:327
  131.0 1.2 reshape.93
  132.4 1.6 copy.75
  134.0 10.7 %all-to-all-done.3.grad.parts = bf16[4,2,512,128]{3,2,1,0:T(8,128)(2,1)S(1)} async-done(((bf16[4,2,512,128]{3,2,1,0:T(8,128)(2,1)}), bf16[4,2,512,128]{3,2,1,0:T(8,128)(2,1)S(1)}, u32[]{:S(2)}, u32[]{:S(2)}) %all-to-all-start.3) | async-done | bytes 1048608 | tf_op jit(solution)/shard_map/all_to_all | solution.py:327
  146.0 4.7 %values_part.1 = bf16[16,64,128]{2,1,0:T(8,128)(2,1)} custom-call(bf16[4,2,512,128]{3,2,1,0:T(8,128)(2,1)} %copy-done, bf16[4,256,512]{2,1,0:T(8,128)(2,1)} %own.1, bf16[4,256,512]{2,1,0:T(8,128)(2,1)} %collective-permute-done.5.near, bf16[4,256,512]{2,1,0:T(8,128)(2,1)} %copy-done.5, bf16[4,256,512]{2,1,0:T(8,128)(2,1)} %collective-permute-done.7.far_near), custom_call_target="tpu_custom_call" | custom-call | tf_op jit(solution)/shard_map/values_part/pallas_call | solution.py:180
  150.8 6.3 %all-to-all-start.4 = ((bf16[16,64,128]{2,1,0:T(8,128)(2,1)}), bf16[16,64,128]{2,1,0:T(8,128)(2,1)S(1)}, u32[]{:S(2)}, u32[]{:S(2)}) async-start(bf16[16,64,128]{2,1,0:T(8,128)(2,1)} %values_part.1), calls=%async_computation.4 | async-start | bytes 524288 | tf_op jit(solution)/shard_map/all_to_all | solution.py:331
  157.0 4.3 %update_all.1 = (bf16[2048,128]{1,0:T(8,128)(2,1)}, f32[2048,128]{1,0:T(8,128)}, f32[2048,128]{1,0:T(8,128)}) custom-call(s32[1]{0:T(128)} %bitcast.t, s32[1]{0:T(128)} %bitcast.1.core, bf16[4,2,512,128]{3,2,1,0:T(8,128)(2,1)} %copy-done, bf16[2048,128]{1,0:T(8,128)(2,1)} %weight.1, f32[2048,128]{1,0:T(8,128)} %one.1, f32[2048,128]{1,0:T(8,128)} %two.1), custom_call_target="tpu_custom_call" | custom-call | tf_op jit(solution)/shard_map/update_all/pallas_call | solution.py:155
  161.3 6.5 %all-to-all-done.4.values = bf16[16,64,128]{2,1,0:T(8,128)(2,1)S(1)} async-done(((bf16[16,64,128]{2,1,0:T(8,128)(2,1)}), bf16[16,64,128]{2,1,0:T(8,128)(2,1)S(1)}, u32[]{:S(2)}, u32[]{:S(2)}) %all-to-all-start.4) | async-done | bytes 262176 | tf_op jit(solution)/shard_map/all_to_all | solution.py:331
  168.5 2.5 %finish_attention.1 = bf16[64,4096]{1,0:T(8,128)(2,1)} custom-call(bf16[16,64,128]{2,1,0:T(8,128)(2,1)} %copy-done.4, f32[4,512,128]{2,1,0:T(8,128)} %bitcast.48, bf16[4,512,64]{2,1,0:T(8,128)(2,1)} %broadcast_select_fusion.spread), custom_call_target="tpu_custom_call" | custom-call | tf_op jit(solution)/shard_map/finish_attention/pallas_call | solution.py:264
  (64 shorter events, 16.9 us)
Async XLA Ops:
  0.6 13.5 %collective-permute-start = (bf16[128,8192]{1,0:T(8,128)(2,1)}, bf16[128,8192]{1,0:T(8,128)(2,1)S(1)}, u32[]{:S(2)}, u32[]{:S(2)}) collective-permute-start(bf16[128,8192]{1,0:T(8,128)(2,1)} %own_1.1), channel_id=1, source_target_pairs={{0,4},{4,0},{1,5},{5,1},{2,6},{6,2},{3,7},{7,3},{8,12},{12,8},{9,1... | collective-permute-start | bytes 6291464 | tf_op jit(solution)/shard_map/ppermute | solution.py:294
  3.2 10.1 %collective-permute-start.1 = (bf16[128,128]{1,0:T(8,128)(2,1)}, bf16[128,128]{1,0:T(8,128)(2,1)S(1)}, u32[]{:S(2)}, u32[]{:S(2)}) collective-permute-start(bf16[128,128]{1,0:T(8,128)(2,1)} %param.12), channel_id=1, source_target_pairs={{0,0},{1,1},{2,2},{3,3},{6,4},{7,5},{4,6},{5,7},{8,8},{9,9},{10,10... | collective-permute-start | bytes 98312 | tf_op jit(solution)/shard_map/ppermute | solution.py:293
  7.4 6.7 %collective-permute-start.2 = (bf16[128,128]{1,0:T(8,128)(2,1)}, bf16[128,128]{1,0:T(8,128)(2,1)S(1)}, u32[]{:S(2)}, u32[]{:S(2)}) collective-permute-start(bf16[128,128]{1,0:T(8,128)(2,1)} %param.12), channel_id=1, source_target_pairs={{4,0},{5,1},{6,2},{7,3},{2,4},{3,5},{0,6},{1,7},{12,8},{13,9},{14,... | collective-permute-start | bytes 98312 | tf_op jit(solution)/shard_map/ppermute | solution.py:293
  9.4 100.9 %collective-permute-start.5 = (bf16[4,256,512]{2,1,0:T(8,128)(2,1)}, bf16[4,256,512]{2,1,0:T(8,128)(2,1)}, u32[]{:S(2)}, u32[]{:S(2)}) collective-permute-start(bf16[4,256,512]{2,1,0:T(8,128)(2,1)} %own.1), channel_id=1, source_target_pairs={{0,1},{1,0},{2,3},{3,2},{4,5},{5,4},{6,7},{7,6},{8,9},{9,8},{10,11... | collective-permute-start | bytes 3145736 | tf_op jit(solution)/shard_map/ppermute | solution.py:324
  13.4 0.8 copy-start.11
  14.1 0.6 copy-start.12
  14.1 1.3 copy-start.1
  18.6 6.9 %copy-start.7 = (bf16[4,16,4096]{2,1,0:T(8,128)(2,1)S(1)}, bf16[4,16,4096]{2,1,0:T(8,128)(2,1)}, u32[]{:S(2)}) copy-start(bf16[4,16,4096]{2,1,0:T(8,128)(2,1)} %param.17) | copy-start | bytes 1572868
  18.6 7.0 %copy-start.10 = (bf16[4,16,512]{2,1,0:T(8,128)(2,1)S(1)}, bf16[4,16,512]{2,1,0:T(8,128)(2,1)}, u32[]{:S(2)}) copy-start(bf16[4,16,512]{2,1,0:T(8,128)(2,1)} %param.18) | copy-start | bytes 196612
  18.6 42.3 %all-to-all-start = ((bf16[8,512,128]{2,1,0:T(8,128)(2,1)}), bf16[8,512,128]{2,1,0:T(8,128)(2,1)S(1)}, u32[]{:S(2)}, u32[]{:S(2)}) async-start(bf16[8,512,128]{2,1,0:T(8,128)(2,1)} %bitcast.47), calls=%async_computation | async-start | bytes 2097152 | tf_op jit(solution)/shard_map/all_to_all | solution.py:300
  25.5 3.1 %copy-start.8 = (bf16[16,32,512]{2,1,0:T(8,128)(2,1)S(1)}, bf16[16,32,512]{2,1,0:T(8,128)(2,1)}, u32[]{:S(2)}) copy-start(bf16[16,32,512]{2,1,0:T(8,128)(2,1)} %param.19) | copy-start | bytes 1572868
  60.9 1.0 copy-start.2
  63.9 25.7 %all-to-all-start.1 = ((bf16[12,48,128]{2,1,0:T(8,128)(2,1)}), bf16[12,48,128]{2,1,0:T(8,128)(2,1)S(1)}, u32[]{:S(2)}, u32[]{:S(2)}) async-start(bf16[12,48,128]{2,1,0:T(8,128)(2,1)} %sum_over_x.1), calls=%async_computation.1 | async-start | bytes 294912 | tf_op jit(solution)/shard_map/all_to_all | solution.py:315
  83.4 6.2 %collective-permute-start.3 = (f32[3,48,128]{2,1,0:T(8,128)S(1)}, f32[3,48,128]{2,1,0:T(8,128)S(1)}, u32[]{:S(2)}, u32[]{:S(2)}) collective-permute-start(f32[3,48,128]{2,1,0:T(8,128)S(1)} %pad_maximum_fusion), channel_id=1, source_target_pairs={{0,0},{1,1},{2,2},{3,3},{6,4},{7,5},{4,6},{5,7},{16,16},{17,17},{1... | collective-permute-start | bytes 221192 | tf_op jit(solution)/shard_map/ppermute | solution.py:309
  89.6 0.6 copy-start.9
  90.2 0.7 copy-start.6
  92.5 5.5 %collective-permute-start.4 = (bf16[48,128]{1,0:T(8,128)(2,1)}, bf16[48,128]{1,0:T(8,128)(2,1)S(1)}, u32[]{:S(2)}, u32[]{:S(2)}) collective-permute-start(bf16[48,128]{1,0:T(8,128)(2,1)} %get-tuple-element.32), channel_id=1, source_target_pairs={{0,0},{1,1},{2,2},{3,3},{4,6},{5,7},{6,4},{7,5},{16,16},{17,17},{1... | collective-permute-start | bytes 36872 | tf_op jit(solution)/shard_map/ppermute | solution.py:321
  99.5 21.9 %all-to-all-start.2 = ((bf16[12,2,48,128]{3,2,1,0:T(8,128)(2,1)}), bf16[12,2,48,128]{3,2,1,0:T(8,128)(2,1)S(1)}, u32[]{:S(2)}, u32[]{:S(2)}) async-start(bf16[12,2,48,128]{3,2,1,0:T(8,128)(2,1)} %broadcast_in_dim.83), calls=%async_computation.2 | async-start | bytes 589824 | tf_op jit(solution)/shard_map/all_to_all | solution.py:323
  108.4 36.3 %collective-permute-start.6 = (bf16[4,256,512]{2,1,0:T(8,128)(2,1)}, bf16[4,256,512]{2,1,0:T(8,128)(2,1)S(1)}, u32[]{:S(2)}, u32[]{:S(2)}) collective-permute-start(bf16[4,256,512]{2,1,0:T(8,128)(2,1)} %own.1), channel_id=1, source_target_pairs={{0,4},{4,0},{1,5},{5,1},{2,6},{6,2},{3,7},{7,3},{8,12},{12,8},{9,1... | collective-permute-start | bytes 3145736 | tf_op jit(solution)/shard_map/ppermute | solution.py:311
  110.3 34.4 %collective-permute-start.7 = (bf16[4,256,512]{2,1,0:T(8,128)(2,1)}, bf16[4,256,512]{2,1,0:T(8,128)(2,1)}, u32[]{:S(2)}, u32[]{:S(2)}) collective-permute-start(bf16[4,256,512]{2,1,0:T(8,128)(2,1)} %collective-permute-done.5.near), channel_id=1, source_target_pairs={{0,4},{4,0},{1,5},{5,1},{2,6},{6,2},{3,7},{7,3},{8,12},{12,8},{9,1... | collective-permute-start | bytes 3145736 | tf_op jit(solution)/shard_map/ppermute | solution.py:328
  121.5 0.7 copy-start.3
  124.2 20.5 %all-to-all-start.3 = ((bf16[4,2,512,128]{3,2,1,0:T(8,128)(2,1)}), bf16[4,2,512,128]{3,2,1,0:T(8,128)(2,1)S(1)}, u32[]{:S(2)}, u32[]{:S(2)}) async-start(bf16[4,2,512,128]{3,2,1,0:T(8,128)(2,1)} %join_parts.1), calls=%async_computation.3 | async-start | bytes 2097152 | tf_op jit(solution)/shard_map/all_to_all | solution.py:327
  144.7 1.0 copy-start
  144.7 1.3 copy-start.5
  150.8 17.0 %all-to-all-start.4 = ((bf16[16,64,128]{2,1,0:T(8,128)(2,1)}), bf16[16,64,128]{2,1,0:T(8,128)(2,1)S(1)}, u32[]{:S(2)}, u32[]{:S(2)}) async-start(bf16[16,64,128]{2,1,0:T(8,128)(2,1)} %values_part.1), calls=%async_computation.4 | async-start | bytes 524288 | tf_op jit(solution)/shard_map/all_to_all | solution.py:331
  167.8 0.7 copy-start.4
where the time goes:
time: 172 us; the launch traced here: 171 us
  starting transfers between devices  62 us (36%)
  waiting for transfers between devices  60.3 us (35%)
  Pallas kernels  20.4 us (12%)
  local copies, waits for them, and re-layouts  18.2 us (11%)
  other arithmetic  4.96 us (3%)
  matrix products  4.23 us (2%)
    all_to_all x1, waiting for transfers between devices, per_device(): lax.all_to_all(parts.reshape(NX * 2, QROWS, 128), (GX, YH), 0, 0, tiled=T...  26.7 us
    all_to_all x1, starting transfers between devices, per_device(): parts = lax.all_to_all(parts, GZ, 0, 0, tiled=True)  14.2 us
    all_to_all x1, waiting for transfers between devices, per_device(): both = lax.all_to_all(both, GX, 0, 0, tiled=True)  10.7 us
    all_to_all x1, starting transfers between devices, per_device(): both = lax.all_to_all(both, GZ, 0, 0, tiled=True)  8.87 us
    all_to_all x1, waiting for transfers between devices, per_device(): both = lax.all_to_all(both, GZ, 0, 0, tiled=True)  8.73 us
    all_to_all x1, starting transfers between devices, per_device(): lax.all_to_all(parts.reshape(NX * 2, QROWS, 128), (GX, YH), 0, 0, tiled=T...  6.89 us
    all_to_all x1, starting transfers between devices, per_device(): both = lax.all_to_all(both, GX, 0, 0, tiled=True)  6.74 us
    all_to_all x1, waiting for transfers between devices, per_device(): values = lax.all_to_all(values, (YH, CO, YL), 0, 0, tiled=True)  6.49 us
  transfers between devices with their start and end apart: 13, of which 7 were waited for; matrix products, arithmetic and copies ran while one was open for 12% of the time, Pallas kernels for 8%

commit v1 on v0

--- a/solution.py
+++ b/solution.py
@@ -82,18 +82,19 @@
 
 
 def sum_x_kernel(parts, out):
-    total = parts[0].astype(jnp.float32)
-    for k in range(1, NX * 2):
-        total = total + parts[k].astype(jnp.float32)
-    total = total.astype(jnp.bfloat16)
-    for z in range(NZ):
-        out[z] = total[STARTS[z] : STARTS[z] + PART]
+    for h in range(2):
+        total = parts[0, h].astype(jnp.float32)
+        for k in range(1, NX):
+            total = total + parts[k, h].astype(jnp.float32)
+        total = total.astype(jnp.bfloat16)
+        for z in range(NZ):
+            out[z, h] = total[STARTS[z] : STARTS[z] + PART]
 
 
 def sum_over_x(parts):
     return pl.pallas_call(
         sum_x_kernel,
-        out_shape=jax.ShapeDtypeStruct((NZ, PART, 128), jnp.bfloat16),
+        out_shape=jax.ShapeDtypeStruct((NZ, 2, PART, 128), jnp.bfloat16),
         in_specs=[vmem()],
         out_specs=vmem(),
         name="sum_over_x",
@@ -102,7 +103,7 @@
 
 def shard_kernel(parts, state, grad_out, weight_out):
     total = parts[0].astype(jnp.float32)
-    for k in range(1, NZ):
+    for k in range(1, NZ * 2):
         total = total + parts[k].astype(jnp.float32)
     grad_out[...] = total.astype(jnp.bfloat16)
     weight_out[...] = apply_adamw(total, state[0], state[1], state[2])[0]
@@ -297,7 +298,7 @@
     queries, new_keys, key_cache, early, parts = lax.optimization_barrier(
         (queries, new_keys, key_cache, early, parts)
     )
-    parts = lax.all_to_all(parts.reshape(NX * 2, QROWS, 128), (GX, YH), 0, 0, tiled=True)
+    parts = lax.all_to_all(parts, GX, 0, 0, tiled=True)
 
     j, i = x // 2, x % 2
     first = (y ^ (2 * (c ^ j)) ^ i) * QROWS + jnp.minimum(PART * z, QROWS - PART)
@@ -308,11 +309,13 @@
     back = [(d, s) for s, d in turn]
     state = lax.ppermute(state, (GX, CO, YL), turn)
 
+    near = lax.ppermute(hidden, YL, [(0, 1), (1, 0), (2, 3), (3, 2)])
+    parts = sum_over_x(parts).reshape(NZ * 2, PART, 128)
+    parts = lax.all_to_all(parts, (GZ, YH), 0, 0, tiled=True)
     far = lax.ppermute(hidden, CO, swap)
+    far_near = lax.ppermute(near, CO, swap)
     cached_probs, fresh_probs = attend_cached(queries, new_keys, key_cache, lengths)
     spread = spread_probs(fresh_probs)
-    parts = sum_over_x(parts)
-    parts = lax.all_to_all(parts, GZ, 0, 0, tiled=True)
     parts, state, cached_probs, spread = lax.optimization_barrier(
         (parts, state, cached_probs, spread)
     )
@@ -321,11 +324,10 @@
     grad = lax.ppermute(grad, (GX, CO, YL), back)
     both = jnp.broadcast_to(jnp.stack([shard, grad])[None], (NZ, 2, PART, 128))
     both = lax.all_to_all(both, GZ, 0, 0, tiled=True)
-    near = lax.ppermute(hidden, YL, [(0, 1), (1, 0), (2, 3), (3, 2)])
     result = weigh_cached(cached_probs, value_cache)
+    both, far, far_near = lax.optimization_barrier((both, far, far_near))
     both = join_parts(both)
     both = lax.all_to_all(both, GX, 0, 0, tiled=True)
-    far_near = lax.ppermute(near, CO, swap)
     both, result = lax.optimization_barrier((both, result))
     values = values_part(both, hidden, near, far, far_near)
     values = lax.all_to_all(values, (YH, CO, YL), 0, 0, tiled=True)

time: 172 us -> 180 us (1.047)
  waiting for transfers between devices: 60.3 us -> 65.9 us
  starting transfers between devices: 62 us -> 66.1 us
    ppermute x1, waiting for transfers between devices: 0.01 us -> 13.9 us  [per_device(): near = lax.ppermute(hidden, YL, [(0, 1), (1, 0), (2, 3), (3, 2)])]
    all_to_all x2, waiting for transfers between devices: 26.7 us -> 13.9 us  [the longest x1 12.8 us: per_device(): parts = lax.all_to_all(parts, GX, 0, 0, tiled=True)]
    all_to_all x1, waiting for transfers between devices: 8.73 us -> 15.6 us  [per_device(): both = lax.all_to_all(both, GZ, 0, 0, tiled=True)]
    all_to_all x1, starting transfers between devices: 6.74 us -> 3.52 us  [per_device(): both = lax.all_to_all(both, GX, 0, 0, tiled=True)]
    broadcast_in_dim x6, local copies, waits for them, and re-layouts: 5.56 us -> 7.78 us  [spread_probs(): spread = jnp.where(same, spread, jnp.zeros((), jnp.bfloat16))]
    ppermute x1, waiting for transfers between devices: 3.51 us -> 1.34 us  [per_device(): grad = lax.ppermute(grad, (GX, CO, YL), back)]
    ppermute x1, starting transfers between devices: 2.01 us -> 4.19 us  [per_device(): grad = lax.ppermute(grad, (GX, CO, YL), back)]
    all_to_all x1, starting transfers between devices: 6.26 us -> 8.35 us  [per_device(): values = lax.all_to_all(values, (YH, CO, YL), 0, 0, tiled=True)]
  transfers between devices with their start and end apart: 13 -> 13, of which waited for: 7 -> 8; matrix products, arithmetic and copies ran while one was open for 12% -> 11% of each run, Pallas kernels for 8% -> 6%
where the time goes in v1:
time: 180 us; the launch traced here: 179 us
  starting transfers between devices  66.1 us (37%)
  waiting for transfers between devices  65.9 us (37%)
  Pallas kernels  20.5 us (11%)
  local copies, waits for them, and re-layouts  16.9 us (9%)
  other arithmetic  4.96 us (3%)
  matrix products  3.21 us (2%)
    all_to_all x1, starting transfers between devices, per_device(): parts = lax.all_to_all(parts, (GZ, YH), 0, 0, tiled=True)  18.7 us
    all_to_all x1, waiting for transfers between devices, per_device(): both = lax.all_to_all(both, GZ, 0, 0, tiled=True)  15.6 us
    ppermute x1, waiting for transfers between devices, per_device(): near = lax.ppermute(hidden, YL, [(0, 1), (1, 0), (2, 3), (3, 2)])  13.9 us
    all_to_all x1, waiting for transfers between devices, per_device(): parts = lax.all_to_all(parts, GX, 0, 0, tiled=True)  12.8 us
    all_to_all x1, waiting for transfers between devices, per_device(): both = lax.all_to_all(both, GX, 0, 0, tiled=True)  12 us
    all_to_all x1, starting transfers between devices, per_device(): values = lax.all_to_all(values, (YH, CO, YL), 0, 0, tiled=True)  8.35 us
    all_to_all x1, starting transfers between devices, per_device(): both = lax.all_to_all(both, GZ, 0, 0, tiled=True)  8.27 us
    broadcast_in_dim x6, local copies, waits for them, and re-layouts, spread_probs(): spread = jnp.where(same, spread, jnp.zeros((), jnp.bfloat16))  7.78 us
  transfers between devices with their start and end apart: 13, of which 8 were waited for; matrix products, arithmetic and copies ran while one was open for 11% of the time, Pallas kernels for 6%

profile of v1, /device:TPU:73, one launch (start us, length us, event | category | flops | bytes accessed | tf_op | source)
XLA Modules:
  0.0 178.6 jit_solution(7906557147423998148)
XLA Ops:
  0.6 2.6 %collective-permute-start = (bf16[128,8192]{1,0:T(8,128)(2,1)}, bf16[128,8192]{1,0:T(8,128)(2,1)S(1)}, u32[]{:S(2)}, u32[]{:S(2)}) collective-permute-start(bf16[128,8192]{1,0:T(8,128)(2,1)} %own_1.1), channel_id=1, source_target_pairs={{0,4},{4,0},{1,5},{5,1},{2,6},{6,2},{3,7},{7,3},{8,12},{12,8},{9,1... | collective-permute-start | bytes 6291464 | tf_op jit(solution)/shard_map/ppermute | solution.py:295
  3.2 2.1 %collective-permute-start.6 = (bf16[4,256,512]{2,1,0:T(8,128)(2,1)}, bf16[4,256,512]{2,1,0:T(8,128)(2,1)}, u32[]{:S(2)}, u32[]{:S(2)}) collective-permute-start(bf16[4,256,512]{2,1,0:T(8,128)(2,1)} %own.1), channel_id=1, source_target_pairs={{0,1},{1,0},{2,3},{3,2},{4,5},{5,4},{6,7},{7,6},{8,9},{9,8},{10,11... | collective-permute-start | bytes 3145736 | tf_op jit(solution)/shard_map/ppermute | solution.py:312
  5.3 4.2 %collective-permute-start.1 = (bf16[128,128]{1,0:T(8,128)(2,1)}, bf16[128,128]{1,0:T(8,128)(2,1)S(1)}, u32[]{:S(2)}, u32[]{:S(2)}) collective-permute-start(bf16[128,128]{1,0:T(8,128)(2,1)} %param.12), channel_id=1, source_target_pairs={{0,0},{1,1},{2,2},{3,3},{6,4},{7,5},{4,6},{5,7},{8,8},{9,9},{10,10... | collective-permute-start | bytes 98312 | tf_op jit(solution)/shard_map/ppermute | solution.py:294
  9.5 1.9 %collective-permute-start.2 = (bf16[128,128]{1,0:T(8,128)(2,1)}, bf16[128,128]{1,0:T(8,128)(2,1)S(1)}, u32[]{:S(2)}, u32[]{:S(2)}) collective-permute-start(bf16[128,128]{1,0:T(8,128)(2,1)} %param.12), channel_id=1, source_target_pairs={{4,0},{5,1},{6,2},{7,3},{2,4},{3,5},{0,6},{1,7},{12,8},{13,9},{14,... | collective-permute-start | bytes 98312 | tf_op jit(solution)/shard_map/ppermute | solution.py:294
  11.5 2.4 %collective-permute-start.5 = (bf16[4,256,512]{2,1,0:T(8,128)(2,1)}, bf16[4,256,512]{2,1,0:T(8,128)(2,1)}, u32[]{:S(2)}, u32[]{:S(2)}) collective-permute-start(bf16[4,256,512]{2,1,0:T(8,128)(2,1)} %own.1), channel_id=1, source_target_pairs={{0,4},{4,0},{1,5},{5,1},{2,6},{6,2},{3,7},{7,3},{8,12},{12,8},{9,1... | collective-permute-start | bytes 3145736 | tf_op jit(solution)/shard_map/ppermute | solution.py:315
  16.3 13.9 %collective-permute-done.6.near = bf16[4,256,512]{2,1,0:T(8,128)(2,1)} collective-permute-done((bf16[4,256,512]{2,1,0:T(8,128)(2,1)}, bf16[4,256,512]{2,1,0:T(8,128)(2,1)}, u32[]{:S(2)}, u32[]{:S(2)}) %collective-permute-start.6) | collective-permute-done | bytes 1048608 | tf_op jit(solution)/shard_map/ppermute | solution.py:312
  30.1 3.1 %collective-permute-start.7 = (bf16[4,256,512]{2,1,0:T(8,128)(2,1)}, bf16[4,256,512]{2,1,0:T(8,128)(2,1)}, u32[]{:S(2)}, u32[]{:S(2)}) collective-permute-start(bf16[4,256,512]{2,1,0:T(8,128)(2,1)} %collective-permute-done.6.near), channel_id=1, source_target_pairs={{0,4},{4,0},{1,5},{5,1},{2,6},{6,2},{3,7},{7,3},{8,12},{12,8},{9,1... | collective-permute-start | bytes 3145736 | tf_op jit(solution)/shard_map/ppermute | solution.py:316
  34.7 3.1 %partial_gradient.1 = bf16[4,2,512,128]{3,2,1,0:T(8,128)(2,1)} custom-call(s32[1]{0:T(128)} %bitcast.t, s32[1]{0:T(128)} %bitcast.1.core, bf16[128,8192]{1,0:T(8,128)(2,1)} %own_1.1, bf16[128,8192]{1,0:T(8,128)(2,1)} %own_1.1, bf16[128,8192]{1,0:T(8,128)(2,1)} %copy-done.1, bf16[128,8192]{1,0:T(8,128)(2,1)} %copy-done.1, bf16[128,128]{1,0:T(8,128)(2,1)} %copy-done.11, ...), custom_call_target="tpu_custom_call" | custom-call | tf_op jit(solution)/shard_map/partial_gradient/pallas_call | solution.py:64
  37.9 2.4 %fusion.6 = f32[16,4,4,4,8]{4,2,3,1,0:T(4,128)S(1)} fusion(bf16[4,16,4,8,128]{4,3,2,1,0:T(8,128)(2,1)S(1)} %bitcast.49, bf16[4,16,4,128,1]{3,2,1,0,4:T(4,128)(2,1)S(1)} %bitcast.57), kind=kOutput, calls=%fused_computation.11 | convolution fusion | flops 2097152 | bytes 622592 | tf_op jit(solution)/shard_map/tnhjd,snhd->nhjts/dot_general | solution.py:209
  41.0 4.0 %all-to-all-start = ((bf16[4,2,512,128]{3,2,1,0:T(8,128)(2,1)}), bf16[4,2,512,128]{3,2,1,0:T(8,128)(2,1)S(1)}, u32[]{:S(2)}, u32[]{:S(2)}) async-start(bf16[4,2,512,128]{3,2,1,0:T(8,128)(2,1)} %partial_gradient.1), calls=%async_computation | async-start | bytes 2097152 | tf_op jit(solution)/shard_map/all_to_all | solution.py:301
  47.2 12.8 %all-to-all-done.parts = bf16[4,2,512,128]{3,2,1,0:T(8,128)(2,1)S(1)} async-done(((bf16[4,2,512,128]{3,2,1,0:T(8,128)(2,1)}), bf16[4,2,512,128]{3,2,1,0:T(8,128)(2,1)S(1)}, u32[]{:S(2)}, u32[]{:S(2)}) %all-to-all-start) | async-done | bytes 1048608 | tf_op jit(solution)/shard_map/all_to_all | solution.py:301
  60.9 2.1 %sum_over_x.1 = bf16[12,2,48,128]{3,2,1,0:T(8,128)(2,1)} custom-call(bf16[4,2,512,128]{3,2,1,0:T(8,128)(2,1)} %copy-done.2), custom_call_target="tpu_custom_call" | custom-call | tf_op jit(solution)/shard_map/sum_over_x/pallas_call | solution.py:95
  63.0 18.7 %all-to-all-start.1 = ((bf16[24,48,128]{2,1,0:T(8,128)(2,1)}), bf16[24,48,128]{2,1,0:T(8,128)(2,1)}, u32[]{:S(2)}, u32[]{:S(2)}) async-start(bf16[24,48,128]{2,1,0:T(8,128)(2,1)} %bitcast.53), calls=%async_computation.1 | async-start | bytes 589824 | tf_op jit(solution)/shard_map/all_to_all | solution.py:314
  83.1 4.2 %broadcast_in_dim.81 = bf16[4,512,64]{1,2,0:T(8,128)(2,1)} reshape(bf16[4,8,4,16,4,16]{3,2,1,5,4,0:T(4,128)(2,1)S(1)} %broadcast_in_dim.80) | data formatting | bytes 524288 | tf_op jit(solution)/shard_map/jit(_where)/broadcast_in_dim | solution.py:235
  87.4 1.2 copy.72
  89.4 2.8 %collective-permute-start.3 = (f32[3,48,128]{2,1,0:T(8,128)S(1)}, f32[3,48,128]{2,1,0:T(8,128)S(1)}, u32[]{:S(2)}, u32[]{:S(2)}) collective-permute-start(f32[3,48,128]{2,1,0:T(8,128)S(1)} %pad_maximum_fusion), channel_id=1, source_target_pairs={{0,0},{1,1},{2,2},{3,3},{6,4},{7,5},{4,6},{5,7},{16,16},{17,17},{1... | collective-permute-start | bytes 221192 | tf_op jit(solution)/shard_map/ppermute | solution.py:310
  93.8 2.7 %collective-permute-done.3.state = f32[3,48,128]{2,1,0:T(8,128)S(1)} collective-permute-done((f32[3,48,128]{2,1,0:T(8,128)S(1)}, f32[3,48,128]{2,1,0:T(8,128)S(1)}, u32[]{:S(2)}, u32[]{:S(2)}) %collective-permute-start.3) | collective-permute-done | bytes 73760 | tf_op jit(solution)/shard_map/ppermute | solution.py:310
  96.5 1.1 all-to-all-done.1.parts
  97.6 1.6 update_shard.1
  99.2 4.2 %collective-permute-start.4 = (bf16[48,128]{1,0:T(8,128)(2,1)}, bf16[48,128]{1,0:T(8,128)(2,1)S(1)}, u32[]{:S(2)}, u32[]{:S(2)}) collective-permute-start(bf16[48,128]{1,0:T(8,128)(2,1)} %get-tuple-element.35), channel_id=1, source_target_pairs={{0,0},{1,1},{2,2},{3,3},{4,6},{5,7},{6,4},{7,5},{16,16},{17,17},{1... | collective-permute-start | bytes 36872 | tf_op jit(solution)/shard_map/ppermute | solution.py:324
  103.4 1.3 collective-permute-done.4
  106.2 8.3 %all-to-all-start.2 = ((bf16[12,2,48,128]{3,2,1,0:T(8,128)(2,1)}), bf16[12,2,48,128]{3,2,1,0:T(8,128)(2,1)S(1)}, u32[]{:S(2)}, u32[]{:S(2)}) async-start(bf16[12,2,48,128]{3,2,1,0:T(8,128)(2,1)} %broadcast_in_dim.83), calls=%async_computation.2 | async-start | bytes 589824 | tf_op jit(solution)/shard_map/all_to_all | solution.py:326
  114.5 15.6 %all-to-all-done.2.parts = bf16[12,2,48,128]{3,2,1,0:T(8,128)(2,1)S(1)} async-done(((bf16[12,2,48,128]{3,2,1,0:T(8,128)(2,1)}), bf16[12,2,48,128]{3,2,1,0:T(8,128)(2,1)S(1)}, u32[]{:S(2)}, u32[]{:S(2)}) %all-to-all-start.2) | async-done | bytes 294944 | tf_op jit(solution)/shard_map/all_to_all | solution.py:326
  130.9 2.1 %join_parts.1 = bf16[4,2,512,128]{3,2,1,0:T(8,128)(2,1)} custom-call(bf16[12,2,48,128]{3,2,1,0:T(8,128)(2,1)} %copy-done.3), custom_call_target="tpu_custom_call" | custom-call | tf_op jit(solution)/shard_map/join_parts/pallas_call | solution.py:132
  132.9 3.5 %all-to-all-start.3 = ((bf16[4,2,512,128]{3,2,1,0:T(8,128)(2,1)}), bf16[4,2,512,128]{3,2,1,0:T(8,128)(2,1)S(1)}, u32[]{:S(2)}, u32[]{:S(2)}) async-start(bf16[4,2,512,128]{3,2,1,0:T(8,128)(2,1)} %join_parts.1), calls=%async_computation.3 | async-start | bytes 2097152 | tf_op jit(solution)/shard_map/all_to_all | solution.py:330
  136.9 1.6 copy.75
  138.5 12.0 %all-to-all-done.3.grad.parts = bf16[4,2,512,128]{3,2,1,0:T(8,128)(2,1)S(1)} async-done(((bf16[4,2,512,128]{3,2,1,0:T(8,128)(2,1)}), bf16[4,2,512,128]{3,2,1,0:T(8,128)(2,1)S(1)}, u32[]{:S(2)}, u32[]{:S(2)}) %all-to-all-start.3) | async-done | bytes 1048608 | tf_op jit(solution)/shard_map/all_to_all | solution.py:330
  151.5 4.7 %values_part.1 = bf16[16,64,128]{2,1,0:T(8,128)(2,1)} custom-call(bf16[4,2,512,128]{3,2,1,0:T(8,128)(2,1)} %copy-done, bf16[4,256,512]{2,1,0:T(8,128)(2,1)} %own.1, bf16[4,256,512]{2,1,0:T(8,128)(2,1)} %collective-permute-done.6.near, bf16[4,256,512]{2,1,0:T(8,128)(2,1)} %collective-permute-done.5.far_own, bf16[4,256,512]{2,1,0:T(8,128)(2,1)} %collective-permute-done.7.far_near), custom_call_target="tpu_custom_call" | custom-call | tf_op jit(solution)/shard_map/values_part/pallas_call | solution.py:181
  156.2 8.4 %all-to-all-start.4 = ((bf16[16,64,128]{2,1,0:T(8,128)(2,1)}), bf16[16,64,128]{2,1,0:T(8,128)(2,1)S(1)}, u32[]{:S(2)}, u32[]{:S(2)}) async-start(bf16[16,64,128]{2,1,0:T(8,128)(2,1)} %values_part.1), calls=%async_computation.4 | async-start | bytes 524288 | tf_op jit(solution)/shard_map/all_to_all | solution.py:333
  164.6 4.3 %update_all.1 = (bf16[2048,128]{1,0:T(8,128)(2,1)}, f32[2048,128]{1,0:T(8,128)}, f32[2048,128]{1,0:T(8,128)}) custom-call(s32[1]{0:T(128)} %bitcast.t, s32[1]{0:T(128)} %bitcast.1.core, bf16[4,2,512,128]{3,2,1,0:T(8,128)(2,1)} %copy-done, bf16[2048,128]{1,0:T(8,128)(2,1)} %weight.1, f32[2048,128]{1,0:T(8,128)} %one.1, f32[2048,128]{1,0:T(8,128)} %two.1), custom_call_target="tpu_custom_call" | custom-call | tf_op jit(solution)/shard_map/update_all/pallas_call | solution.py:156
  168.9 6.5 %all-to-all-done.4.values = bf16[16,64,128]{2,1,0:T(8,128)(2,1)S(1)} async-done(((bf16[16,64,128]{2,1,0:T(8,128)(2,1)}), bf16[16,64,128]{2,1,0:T(8,128)(2,1)S(1)}, u32[]{:S(2)}, u32[]{:S(2)}) %all-to-all-start.4) | async-done | bytes 262176 | tf_op jit(solution)/shard_map/all_to_all | solution.py:333
  176.1 2.5 %finish_attention.1 = bf16[64,4096]{1,0:T(8,128)(2,1)} custom-call(bf16[16,64,128]{2,1,0:T(8,128)(2,1)} %copy-done.4, f32[4,512,128]{2,1,0:T(8,128)} %bitcast.47, bf16[4,512,64]{2,1,0:T(8,128)(2,1)} %broadcast_select_fusion.spread), custom_call_target="tpu_custom_call" | custom-call | tf_op jit(solution)/shard_map/finish_attention/pallas_call | solution.py:265
  (64 shorter events, 15.7 us)
Async XLA Ops:
  0.6 32.7 %collective-permute-start = (bf16[128,8192]{1,0:T(8,128)(2,1)}, bf16[128,8192]{1,0:T(8,128)(2,1)S(1)}, u32[]{:S(2)}, u32[]{:S(2)}) collective-permute-start(bf16[128,8192]{1,0:T(8,128)(2,1)} %own_1.1), channel_id=1, source_target_pairs={{0,4},{4,0},{1,5},{5,1},{2,6},{6,2},{3,7},{7,3},{8,12},{12,8},{9,1... | collective-permute-start | bytes 6291464 | tf_op jit(solution)/shard_map/ppermute | solution.py:295
  3.2 26.9 %collective-permute-start.6 = (bf16[4,256,512]{2,1,0:T(8,128)(2,1)}, bf16[4,256,512]{2,1,0:T(8,128)(2,1)}, u32[]{:S(2)}, u32[]{:S(2)}) collective-permute-start(bf16[4,256,512]{2,1,0:T(8,128)(2,1)} %own.1), channel_id=1, source_target_pairs={{0,1},{1,0},{2,3},{3,2},{4,5},{5,4},{6,7},{7,6},{8,9},{9,8},{10,11... | collective-permute-start | bytes 3145736 | tf_op jit(solution)/shard_map/ppermute | solution.py:312
  5.3 28.0 %collective-permute-start.1 = (bf16[128,128]{1,0:T(8,128)(2,1)}, bf16[128,128]{1,0:T(8,128)(2,1)S(1)}, u32[]{:S(2)}, u32[]{:S(2)}) collective-permute-start(bf16[128,128]{1,0:T(8,128)(2,1)} %param.12), channel_id=1, source_target_pairs={{0,0},{1,1},{2,2},{3,3},{6,4},{7,5},{4,6},{5,7},{8,8},{9,9},{10,10... | collective-permute-start | bytes 98312 | tf_op jit(solution)/shard_map/ppermute | solution.py:294
  9.5 23.8 %collective-permute-start.2 = (bf16[128,128]{1,0:T(8,128)(2,1)}, bf16[128,128]{1,0:T(8,128)(2,1)S(1)}, u32[]{:S(2)}, u32[]{:S(2)}) collective-permute-start(bf16[128,128]{1,0:T(8,128)(2,1)} %param.12), channel_id=1, source_target_pairs={{4,0},{5,1},{6,2},{7,3},{2,4},{3,5},{0,6},{1,7},{12,8},{13,9},{14,... | collective-permute-start | bytes 98312 | tf_op jit(solution)/shard_map/ppermute | solution.py:294
  11.5 103.0 %collective-permute-start.5 = (bf16[4,256,512]{2,1,0:T(8,128)(2,1)}, bf16[4,256,512]{2,1,0:T(8,128)(2,1)}, u32[]{:S(2)}, u32[]{:S(2)}) collective-permute-start(bf16[4,256,512]{2,1,0:T(8,128)(2,1)} %own.1), channel_id=1, source_target_pairs={{0,4},{4,0},{1,5},{5,1},{2,6},{6,2},{3,7},{7,3},{8,12},{12,8},{9,1... | collective-permute-start | bytes 3145736 | tf_op jit(solution)/shard_map/ppermute | solution.py:315
  30.1 84.4 %collective-permute-start.7 = (bf16[4,256,512]{2,1,0:T(8,128)(2,1)}, bf16[4,256,512]{2,1,0:T(8,128)(2,1)}, u32[]{:S(2)}, u32[]{:S(2)}) collective-permute-start(bf16[4,256,512]{2,1,0:T(8,128)(2,1)} %collective-permute-done.6.near), channel_id=1, source_target_pairs={{0,4},{4,0},{1,5},{5,1},{2,6},{6,2},{3,7},{7,3},{8,12},{12,8},{9,1... | collective-permute-start | bytes 3145736 | tf_op jit(solution)/shard_map/ppermute | solution.py:316
  33.3 0.6 copy-start.11
  33.3 0.6 copy-start.12
  33.3 1.3 copy-start.1
  34.6 3.1 %copy-start.5 = (bf16[4,16,4096]{2,1,0:T(8,128)(2,1)S(1)}, bf16[4,16,4096]{2,1,0:T(8,128)(2,1)}, u32[]{:S(2)}) copy-start(bf16[4,16,4096]{2,1,0:T(8,128)(2,1)} %param.17) | copy-start | bytes 1572868
  34.7 3.2 %copy-start.10 = (bf16[4,16,512]{2,1,0:T(8,128)(2,1)S(1)}, bf16[4,16,512]{2,1,0:T(8,128)(2,1)}, u32[]{:S(2)}) copy-start(bf16[4,16,512]{2,1,0:T(8,128)(2,1)} %param.18) | copy-start | bytes 196612
  37.8 3.1 %copy-start.6 = (bf16[16,32,512]{2,1,0:T(8,128)(2,1)S(1)}, bf16[16,32,512]{2,1,0:T(8,128)(2,1)}, u32[]{:S(2)}) copy-start(bf16[16,32,512]{2,1,0:T(8,128)(2,1)} %param.19) | copy-start | bytes 1572868
  41.0 18.9 %all-to-all-start = ((bf16[4,2,512,128]{3,2,1,0:T(8,128)(2,1)}), bf16[4,2,512,128]{3,2,1,0:T(8,128)(2,1)S(1)}, u32[]{:S(2)}, u32[]{:S(2)}) async-start(bf16[4,2,512,128]{3,2,1,0:T(8,128)(2,1)} %partial_gradient.1), calls=%async_computation | async-start | bytes 2097152 | tf_op jit(solution)/shard_map/all_to_all | solution.py:301
  59.9 1.0 copy-start.2
  63.0 34.6 %all-to-all-start.1 = ((bf16[24,48,128]{2,1,0:T(8,128)(2,1)}), bf16[24,48,128]{2,1,0:T(8,128)(2,1)}, u32[]{:S(2)}, u32[]{:S(2)}) async-start(bf16[24,48,128]{2,1,0:T(8,128)(2,1)} %bitcast.53), calls=%async_computation.1 | async-start | bytes 589824 | tf_op jit(solution)/shard_map/all_to_all | solution.py:314
  83.1 9.8 %copy-start.8 = (pred[512,64]{1,0:T(8,128)(4,1)S(1)}, pred[512,64]{1,0:T(8,128)(4,1)}, u32[]{:S(2)}) copy-start(pred[512,64]{1,0:T(8,128)(4,1)} %copy.68) | copy-start | bytes 98308
  89.4 7.1 %collective-permute-start.3 = (f32[3,48,128]{2,1,0:T(8,128)S(1)}, f32[3,48,128]{2,1,0:T(8,128)S(1)}, u32[]{:S(2)}, u32[]{:S(2)}) collective-permute-start(f32[3,48,128]{2,1,0:T(8,128)S(1)} %pad_maximum_fusion), channel_id=1, source_target_pairs={{0,0},{1,1},{2,2},{3,3},{6,4},{7,5},{4,6},{5,7},{16,16},{17,17},{1... | collective-permute-start | bytes 221192 | tf_op jit(solution)/shard_map/ppermute | solution.py:310
  96.5 1.1 copy-start.9
  99.2 5.5 %collective-permute-start.4 = (bf16[48,128]{1,0:T(8,128)(2,1)}, bf16[48,128]{1,0:T(8,128)(2,1)S(1)}, u32[]{:S(2)}, u32[]{:S(2)}) collective-permute-start(bf16[48,128]{1,0:T(8,128)(2,1)} %get-tuple-element.35), channel_id=1, source_target_pairs={{0,0},{1,1},{2,2},{3,3},{4,6},{5,7},{6,4},{7,5},{16,16},{17,17},{1... | collective-permute-start | bytes 36872 | tf_op jit(solution)/shard_map/ppermute | solution.py:324
  105.5 31.0 %copy-start.7 = (bf16[16,32,512]{2,1,0:T(8,128)(2,1)S(1)}, bf16[16,32,512]{2,1,0:T(8,128)(2,1)}, u32[]{:S(2)}) copy-start(bf16[16,32,512]{2,1,0:T(8,128)(2,1)} %param.20) | copy-start | bytes 1572868
  106.2 23.9 %all-to-all-start.2 = ((bf16[12,2,48,128]{3,2,1,0:T(8,128)(2,1)}), bf16[12,2,48,128]{3,2,1,0:T(8,128)(2,1)S(1)}, u32[]{:S(2)}, u32[]{:S(2)}) async-start(bf16[12,2,48,128]{3,2,1,0:T(8,128)(2,1)} %broadcast_in_dim.83), calls=%async_computation.2 | async-start | bytes 589824 | tf_op jit(solution)/shard_map/all_to_all | solution.py:326
  130.1 0.7 copy-start.3
  132.9 17.6 %all-to-all-start.3 = ((bf16[4,2,512,128]{3,2,1,0:T(8,128)(2,1)}), bf16[4,2,512,128]{3,2,1,0:T(8,128)(2,1)S(1)}, u32[]{:S(2)}, u32[]{:S(2)}) async-start(bf16[4,2,512,128]{3,2,1,0:T(8,128)(2,1)} %join_parts.1), calls=%async_computation.3 | async-start | bytes 2097152 | tf_op jit(solution)/shard_map/all_to_all | solution.py:330
  150.5 1.0 copy-start
  156.2 19.1 %all-to-all-start.4 = ((bf16[16,64,128]{2,1,0:T(8,128)(2,1)}), bf16[16,64,128]{2,1,0:T(8,128)(2,1)S(1)}, u32[]{:S(2)}, u32[]{:S(2)}) async-start(bf16[16,64,128]{2,1,0:T(8,128)(2,1)} %values_part.1), calls=%async_computation.4 | async-start | bytes 524288 | tf_op jit(solution)/shard_map/all_to_all | solution.py:333
  175.4 0.7 copy-start.4
